TPU v7x, 32 devices: a whole 2x2x4 slice. The times are simulated.
32 devices in a mesh: node: 4 (over z), local: 8 (over y, x, core).
Axes of the slice: x: 2, y: 2, z: 4, core: 2. Of those that a mesh axis runs over, the one named last changes fastest.
Arguments:
- x: bfloat16 [64, 128, 512], P(('node', 'local'))
- y_cot: bfloat16 [64, 128, 512], P(('node', 'local'))
- ln1_gain: bfloat16 [2, 512], P(None, ('node', 'local'))
- ln1_bias: bfloat16 [2, 512], P(None, ('node', 'local'))
- qkv_weight: bfloat16 [2, 512, 8, 192], P(None, ('node', 'local'))
- qkv_bias: bfloat16 [2, 1536], P(None, ('node', 'local'))
- out_weight: bfloat16 [2, 512, 512], P(None, ('node', 'local'))
- out_bias: bfloat16 [2, 512], P(None, ('node', 'local'))
- ln2_gain: bfloat16 [2, 512], P(None, ('node', 'local'))
- ln2_bias: bfloat16 [2, 512], P(None, ('node', 'local'))
- up_weight: bfloat16 [2, 512, 2048], P(None, ('node', 'local'))
- up_bias: bfloat16 [2, 2048], P(None, ('node', 'local'))
- down_weight: bfloat16 [2, 2048, 512], P(None, ('node', 'local'))
- down_bias: bfloat16 [2, 512], P(None, ('node', 'local'))
Outputs:
- output 1: bfloat16 [64, 128, 512], P(('node', 'local'))
- output 2: bfloat16 [64, 128, 512], P(('node', 'local'))
- output 3: bfloat16 [2, 512], P(None, ('node', 'local'))
- output 4: bfloat16 [2, 512], P(None, ('node', 'local'))
- output 5: bfloat16 [2, 512, 8, 192], P(None, ('node', 'local'))
- output 6: bfloat16 [2, 1536], P(None, ('node', 'local'))
- output 7: bfloat16 [2, 512, 512], P(None, ('node', 'local'))
- output 8: bfloat16 [2, 512], P(None, ('node', 'local'))
- output 9: bfloat16 [2, 512], P(None, ('node', 'local'))
- output 10: bfloat16 [2, 512], P(None, ('node', 'local'))
- output 11: bfloat16 [2, 512, 2048], P(None, ('node', 'local'))
- output 12: bfloat16 [2, 2048], P(None, ('node', 'local'))
- output 13: bfloat16 [2, 2048, 512], P(None, ('node', 'local'))
- output 14: bfloat16 [2, 512], P(None, ('node', 'local'))
All inputs are finite; a program needn't handle non-finite values.
Results may differ from a plain program's by a relative error of at most 0.017538.
Values are sent between devices in bfloat16 or wider.
A program may use at most 1 GiB of HBM per device.

v0:
```python
import functools
import jax
import numpy as np
import jax.numpy as jnp
from jax import lax
from jax.experimental import pallas as pl
from jax.experimental.pallas import tpu as pltpu
from jax.sharding import PartitionSpec as P

EPSILON = 1e-5
MESH = pl.DeviceIdType.MESH
LAYERS = 2
ROWS = 16
SMALL = 16


def positions():
    z = lax.axis_index('node')
    l = lax.axis_index('local')
    c = l % 2
    x = (l // 2) % 2
    y = l // 4
    partner = (z, l + 1 - 2 * c)
    x_nbr = (z, l + 2 - 4 * x)
    y_nbr = (z, (l + 4) % 8)
    z_others = [z + 1 - 2 * (z % 2), (z + 2) % 4, 3 - z]
    return z, l, c, x, y, partner, x_nbr, y_nbr, z_others


def entry_barrier(pos):
    z, l, c, x, y, partner, x_nbr, y_nbr, z_others = pos
    barrier = pltpu.get_barrier_semaphore()
    for dev in [partner, x_nbr, y_nbr] + [(zo, l) for zo in z_others]:
        pl.semaphore_signal(barrier, inc=1, device_id=dev, device_id_type=MESH)
    pl.semaphore_wait(barrier, 6)


class Copies:
    def __init__(self, send_sems, recv_sems):
        self.send_sems, self.recv_sems, self.used = send_sems, recv_sems, 0
        self.open_sends = []

    def make(self, src, dst, dev):
        idx = self.used
        self.used += 1
        return pltpu.make_async_remote_copy(src_ref=src, dst_ref=dst, send_sem=self.send_sems.at[idx],
                                            recv_sem=self.recv_sems.at[idx], device_id=dev, device_id_type=MESH)

    def start(self, src, dst, dev):
        copy = self.make(src, dst, dev)
        copy.start()
        self.open_sends.append(copy)
        return copy

    def finish(self):
        for copy in self.open_sends:
            copy.wait_send()
        self.open_sends = []


def small_reduce_steps(copies, pos, src, bufs, out):
    z, l, c, x, y, partner, x_nbr, y_nbr, z_others = pos
    held = src
    for step, dev in enumerate((partner, x_nbr, y_nbr)):
        copy = copies.start(held, bufs.at[2 * step], dev)
        yield
        copy.wait_recv()
        bufs[2 * step + 1] = held[...] + bufs[2 * step]
        held = bufs.at[2 * step + 1]
    sends = [copies.start(held, bufs.at[6 + k], (zo, l)) for k, zo in enumerate(z_others)]
    yield
    for copy in sends:
        copy.wait_recv()
    out[...] = (held[...] + bufs[6]) + (bufs[7] + bufs[8])
    yield


def gather_steps(copies, pos, own, full, lo, width):
    z, l, c, x, y, partner, x_nbr, y_nbr, z_others = pos
    half = width // 2
    cols, cols_a, cols_b = pl.ds(lo, width), pl.ds(lo, half), pl.ds(lo + half, half)
    after = ((z + 1) % 4, l)
    z_order = [z, (z + 3) % 4, (z + 2) % 4, (z + 1) % 4]

    def block(zz, yy, xx, cc):
        return full.at[zz, yy, xx, cc, :, cols]

    from_z, from_x, from_y, diag, to_partner = [None] * 4, [None] * 4, [None] * 4, [], []

    def spread(k, got, place):
        if k < 3:
            from_z[k + 1] = copies.start(got, place, after)
        from_x[k] = copies.start(got, place, x_nbr)
        from_y[k] = copies.start(got, place, y_nbr)

    def forward_z(k):
        from_z[k].wait_recv()
        got = block(z_order[k], y, x, c)
        spread(k, got, got)

    def forward_cross(k):
        zz = z_order[k]
        from_x[k].wait_recv()
        got = full.at[zz, y, 1 - x, c, :, cols_a]
        diag.append(copies.start(got, got, y_nbr))
        from_y[k].wait_recv()
        got = full.at[zz, 1 - y, x, c, :, cols_b]
        diag.append(copies.start(got, got, x_nbr))

    def forward_partner(yy, xx):
        got = full.at[:, yy, xx, c, :, cols]
        to_partner.append(copies.start(got, got, partner))

    spread(0, own.at[:, cols], block(z, y, x, c))
    full[z, y, x, c, :, cols] = own[:, cols]
    yield
    forward_z(1)
    yield
    forward_cross(0)
    yield
    forward_z(2)
    yield
    forward_cross(1)
    yield
    forward_z(3)
    forward_partner(y, x)
    yield
    forward_cross(2)
    yield
    forward_cross(3)
    forward_partner(y, 1 - x)
    forward_partner(1 - y, x)
    yield
    for copy in diag:
        copy.wait_recv()
    forward_partner(1 - y, 1 - x)
    yield
    for copy in to_partner:
        copy.wait_recv()
    yield


STEP_TIMES = (0, 4, 4.5, 8, 8.5, 12, 13, 16, 19, 22)


def gather_program(pieces, starts, small_gen, done):
    events = [(start + time, i, step) for i, start in enumerate(starts) for step, time in enumerate(STEP_TIMES)]
    events += [(time, -1, step) for step, time in enumerate((0.5, 3, 6, 8, 11))]
    for _, i, step in sorted(events):
        if i < 0:
            next(small_gen)
        else:
            next(pieces[i])
            if step + 1 == len(STEP_TIMES):
                done.append(i)
        yield


def scatter_chunk_steps(copies, pos, grads, part0, partx, party, last, partz, out, lo, width):
    z, l, c, x, y, partner, x_nbr, y_nbr, z_others = pos
    half = width // 2
    cols, cols_a, cols_b = pl.ds(lo, width), pl.ds(lo, half), pl.ds(lo + half, half)
    hcols = pl.ds(lo // 2, half)
    swap = copies.make(grads.at[:, :, :, 1 - c, :, cols], part0.at[:, :, :, :, cols], partner)
    swap.start()
    yield
    swap.wait()
    part0[:, :, :, :, cols] = part0[:, :, :, :, cols] + grads[:, :, :, c, :, cols]
    send_a = copies.start(part0.at[:, :, 1 - x, :, cols_a], partx.at[:, :, :, hcols], x_nbr)
    send_b = copies.start(part0.at[:, 1 - y, :, :, cols_b], party.at[:, :, :, hcols], y_nbr)
    yield
    send_a.wait_recv()
    partx[:, :, :, hcols] = partx[:, :, :, hcols] + part0[:, :, x, :, cols_a]
    send_a = copies.start(partx.at[:, 1 - y, :, hcols], last.at[:, :, cols_a], y_nbr)
    send_b.wait_recv()
    party[:, :, :, hcols] = party[:, :, :, hcols] + part0[:, y, :, :, cols_b]
    send_b = copies.start(party.at[:, 1 - x, :, hcols], last.at[:, :, cols_b], x_nbr)
    yield
    send_a.wait_recv()
    send_b.wait_recv()
    last[:, :, cols_a] = last[:, :, cols_a] + partx[:, y, :, hcols]
    last[:, :, cols_b] = last[:, :, cols_b] + party[:, x, :, hcols]
    sends = [copies.start(last.at[zo, :, cols], partz.at[k, :, cols], (zo, l)) for k, zo in enumerate(z_others)]
    yield
    for copy in sends:
        copy.wait_recv()
    total = (last[z, :, cols] + partz[0, :, cols]) + (partz[1, :, cols] + partz[2, :, cols])
    out[:, cols] = total.astype(out.dtype)
    yield


class ScatterQueue:
    def __init__(self):
        self.waiting = [[], [], [], []]

    def add(self, chunk):
        next(chunk)
        self.waiting[0].append(chunk)

    def pump(self, *stages):
        for stage in stages:
            if self.waiting[stage]:
                chunk = self.waiting[stage].pop(0)
                next(chunk)
                if stage < 3:
                    self.waiting[stage + 1].append(chunk)

    def drain(self, lag, between):
        while any(self.waiting):
            next(between, None)
            for stage in range(4):
                if len(self.waiting[stage]) >= lag or not any(self.waiting[:stage]):
                    self.pump(stage)


def dot(first, second):
    return lax.dot_general(first, second, (((1,), (0,)), ((), ())), preferred_element_type=jnp.float32)


def dot_bt(first, second):
    return lax.dot_general(first, second, (((1,), (1,)), ((), ())), preferred_element_type=jnp.float32)


def dot_at(first, second):
    return lax.dot_general(first, second, (((0,), (0,)), ((), ())), preferred_element_type=jnp.float32)


WIDE = 512
PAIR = 128
SEQ = 128
OUT, UP, ACOLS = 3 * WIDE, 4 * WIDE, 8 * WIDE


def normalised(hidden32):
    center = hidden32 - jnp.mean(hidden32, axis=-1, keepdims=True)
    rstd = lax.rsqrt(jnp.mean(center * center, axis=-1, keepdims=True) + EPSILON)
    return center * rstd, rstd


def weight(full, layer, lo, width=WIDE):
    return full[layer, :, :, :, :, :, lo:lo + width].reshape(WIDE, width)


def down_weight_part(full, layer, k):
    return full[layer, k].reshape(WIDE, WIDE)


def rotate(piece, tab):
    piece = piece.reshape(-1, SEQ, PAIR)
    up, down = pltpu.roll(piece, PAIR - 8, 2), pltpu.roll(piece, 8, 2)
    return (piece * tab[0] + up * tab[1] + down * tab[2]).reshape(-1, PAIR)


def rotate_back(piece, tab):
    piece = piece.reshape(-1, SEQ, PAIR)
    turned = (piece * tab[0] + pltpu.roll(piece * tab[1], 8, 2) + pltpu.roll(piece * tab[2], PAIR - 8, 2))
    return turned.reshape(-1, PAIR)


def low_half(rows):
    return lax.broadcasted_iota(jnp.int32, (rows, PAIR), 1) < PAIR // 2


def head_masks():
    first = low_half(SEQ)
    return (jnp.where(first, 1.0, 0.0).astype(jnp.bfloat16), jnp.where(first, 0.0, 1.0).astype(jnp.bfloat16))


def attention_blocks(tokens):
    for s in range(tokens // SEQ):
        for j in range(WIDE // PAIR):
            yield s, j, pl.ds(s * SEQ, SEQ), pl.ds(j * PAIR, PAIR)


def layer_forward(layer, hidden, weights, small, tab, saved, hooks):
    n1, n2, qkv, probs, ctx, slope, act, d_qkv = saved
    wide_w, down_w = weights
    tokens = hidden.shape[0]

    def vec(row):
        return small[pl.ds(layer * SMALL + row, 1), :]

    hidden32 = hidden[...].astype(jnp.float32)
    scaled, _ = normalised(hidden32)
    n1[...] = (scaled * vec(0) + vec(1)).astype(jnp.bfloat16)
    n2[...] = (scaled * vec(3) + vec(4)).astype(jnp.bfloat16)
    hooks('norm')
    low = low_half(tokens)
    qkv_bias = jnp.concatenate([vec(10), vec(11), vec(12)], axis=1)
    group = 6 * PAIR
    for i in range(2):
        part = dot(n1[...], weight(wide_w, layer, i * group, group)) + qkv_bias[:, i * group:(i + 1) * group]
        for jj in range(2):
            first, second, third = (part[:, (3 * jj + m) * PAIR:(3 * jj + m + 1) * PAIR] for m in range(3))
            cols = pl.ds((2 * i + jj) * PAIR, PAIR)
            query = jnp.where(low, first, second)
            key = jnp.where(low, pltpu.roll(first, PAIR // 2, 1), pltpu.roll(third, PAIR // 2, 1))
            qkv[0, :, cols] = rotate(query, tab).astype(jnp.bfloat16)
            qkv[1, :, cols] = rotate(key, tab).astype(jnp.bfloat16)
            qkv[2, :, cols] = jnp.where(low, second, third).astype(jnp.bfloat16)
    hooks('qkv')
    causal = (lax.broadcasted_iota(jnp.int32, (SEQ, SEQ), 0) >= lax.broadcasted_iota(jnp.int32, (SEQ, SEQ), 1))
    masks, low = head_masks(), low_half(SEQ)
    for s, j, rows, cols in attention_blocks(tokens):
        query, key, value = qkv[0, rows, cols], qkv[1, rows, cols], qkv[2, rows, cols]
        heads = []
        for h in range(2):
            scores = dot_bt(query * masks[h], key) * 0.125
            scores = jnp.where(causal, scores, -1e30)
            attn = jnp.exp(scores - jnp.max(scores, axis=-1, keepdims=True))
            attn = attn / jnp.sum(attn, axis=-1, keepdims=True)
            probs[s, j, h] = attn
            heads.append(dot(attn.astype(jnp.bfloat16), value))
        ctx[rows, cols] = jnp.where(low, heads[0], heads[1]).astype(jnp.bfloat16)
        if j == 3:
            hooks('attn')
    total = hidden32 + (dot(ctx[...], weight(wide_w, layer, OUT)) + vec(2))
    hooks('out')
    mlp = None
    for k in range(4):
        pre = dot(n2[...], weight(wide_w, layer, UP + k * WIDE)) + vec(6 + k)
        bell = lax.erf(pre * 0.7071067811865476) + 1.0
        act[:, k * WIDE:(k + 1) * WIDE] = (0.5 * pre * bell).astype(jnp.bfloat16)
        slope[:, k * WIDE:(k + 1) * WIDE] = 0.5 * bell + pre * (jnp.exp(-0.5 * pre * pre) * 0.3989422804014327)
        if k == 0:
            hooks('up')
        term = dot(act[:, k * WIDE:(k + 1) * WIDE], down_weight_part(down_w, layer, k))
        mlp = term if mlp is None else mlp + term
        hooks('mlp')
    return (total + (mlp + vec(5))).astype(jnp.bfloat16)


def layer_backward(layer, hidden, d_out, weights, small, tab, saved, grads, small_grads, hooks):
    n1, n2, qkv, probs, ctx, slope, act, d_qkv = saved
    wide_w, down_w = weights
    wide_g, down_g = grads
    tokens = hidden.shape[0]

    def vec(row):
        return small[pl.ds(layer * SMALL + row, 1), :]

    def put_small(row, value):
        small_grads[pl.ds(layer * SMALL + row, 1), :] = jnp.sum(value, axis=0, keepdims=True)

    def put(lo, value):
        wide_g[:, :, :, :, :, lo:lo + WIDE] = value.reshape(wide_g.shape[:5] + (WIDE,))

    d_out32 = d_out[...].astype(jnp.float32)
    put_small(2, d_out32)
    put_small(5, d_out32)
    half = WIDE // 2
    for k in range(2):
        value = dot_at(act[...], d_out[:, k * half:(k + 1) * half])
        down_g[:, :, :, :, :, k * half:(k + 1) * half] = value.reshape(down_g.shape[:5] + (half,))
        hooks('down', (1, k * half))
    d_n2 = None
    for k in range(4):
        d_act = dot_bt(d_out[...], down_weight_part(down_w, layer, k)).astype(jnp.bfloat16)
        d_pre = d_act.astype(jnp.float32) * slope[:, k * WIDE:(k + 1) * WIDE]
        put_small(6 + k, d_pre)
        act[:, k * WIDE:(k + 1) * WIDE] = d_pre.astype(jnp.bfloat16)
        d_pre_bf = act[:, k * WIDE:(k + 1) * WIDE]
        put(UP + k * WIDE, dot_at(n2[...], d_pre_bf))
        term = dot_bt(d_pre_bf, weight(wide_w, layer, UP + k * WIDE))
        d_n2 = term if d_n2 is None else d_n2 + term
        if k % 2:
            hooks('up', (0, UP + (k - 1) * WIDE))
    d_n2 = d_n2.astype(jnp.bfloat16)
    put(OUT, dot_at(ctx[...], d_out[...]))
    ctx[...] = dot_bt(d_out[...], weight(wide_w, layer, OUT)).astype(jnp.bfloat16)
    hooks('dctx')
    masks, low = head_masks(), low_half(SEQ)
    for s, j, rows, cols in attention_blocks(tokens):
        query, key, value = qkv[0, rows, cols], qkv[1, rows, cols], qkv[2, rows, cols]
        d_ctx = ctx[rows, cols]
        d_q, d_k, d_v = [], [], []
        for h in range(2):
            attn = probs[s, j, h]
            d_probs = dot_bt(d_ctx * masks[h], value).astype(jnp.bfloat16).astype(jnp.float32)
            d_v.append(dot_at(attn.astype(jnp.bfloat16), d_ctx))
            inner = jnp.sum(d_probs * attn, axis=-1, keepdims=True)
            d_scores = (attn * (d_probs - inner) * 0.125).astype(jnp.bfloat16)
            d_q.append(dot(d_scores, key))
            d_k.append(dot_at(d_scores, query))
        qkv[0, rows, cols] = jnp.where(low, d_q[0], d_q[1]).astype(jnp.bfloat16)
        qkv[1, rows, cols] = jnp.where(low, d_k[0], d_k[1]).astype(jnp.bfloat16)
        qkv[2, rows, cols] = jnp.where(low, d_v[0], d_v[1]).astype(jnp.bfloat16)
        if j == 3:
            hooks('dattn')
    low = low_half(tokens)
    for j in range(WIDE // PAIR):
        cols = pl.ds(j * PAIR, PAIR)
        d_query, d_key, d_value = (qkv[t, :, cols].astype(jnp.float32) for t in range(3))
        d_query = rotate_back(d_query, tab)
        d_key = pltpu.roll(rotate_back(d_key, tab), PAIR // 2, 1)
        parts = (jnp.where(low, d_query, d_key), jnp.where(low, d_value, d_query), jnp.where(low, d_key, d_value))
        for m, part in enumerate(parts):
            lo = (3 * j + m) * PAIR
            row = layer * SMALL + 10 + lo // WIDE
            small_grads[pl.ds(row, 1), pl.ds(lo % WIDE, PAIR)] = jnp.sum(part, axis=0, keepdims=True)
            d_qkv[:, lo:lo + PAIR] = part.astype(jnp.bfloat16)
    d_n1 = None
    for t in (2, 1, 0):
        piece = d_qkv[:, t * WIDE:(t + 1) * WIDE]
        put(t * WIDE, dot_at(n1[...], piece))
        term = dot_bt(piece, weight(wide_w, layer, t * WIDE))
        d_n1 = term if d_n1 is None else d_n1 + term
        if t != 1:
            hooks('dqkv', (0, (t // 2) * 2 * WIDE))
    d_n1 = d_n1.astype(jnp.bfloat16).astype(jnp.float32)
    d_n2 = d_n2.astype(jnp.float32)
    scaled, rstd = normalised(hidden[...].astype(jnp.float32))
    put_small(0, d_n1 * scaled)
    put_small(1, d_n1)
    put_small(3, d_n2 * scaled)
    put_small(4, d_n2)
    d_scaled = d_n1 * vec(0) + d_n2 * vec(3)
    d_hidden = rstd * (d_scaled - jnp.mean(d_scaled, axis=-1, keepdims=True)
                       - scaled * jnp.mean(d_scaled * scaled, axis=-1, keepdims=True))
    return (d_out32 + d_hidden).astype(jnp.bfloat16)


def places(rank, part, width):
    shift = lax.broadcasted_iota(jnp.int32, (part, width), 1) - lax.broadcasted_iota(jnp.int32, (part, width), 0)
    return jnp.where(shift == rank * part, 1.0, 0.0).astype(jnp.bfloat16)


VECTOR_ROWS = ((0, 1), (1, 1), (10, 3), (2, 1), (3, 1), (4, 1), (6, 4), (5, 1))


def place_small(rank, vectors, small_own):
    small_own[...] = jnp.zeros_like(small_own)
    for ref, (row, count) in zip(vectors, VECTOR_ROWS):
        wide = dot(ref[...], places(rank, ref.shape[1], count * WIDE))
        for layer in range(LAYERS):
            for i in range(count):
                small_own[pl.ds(layer * SMALL + row + i, 1), :] = wide[layer:layer + 1, i * WIDE:(i + 1) * WIDE]


def step_kernel(x, y_cot, qkv_own, out_own, up_own, down_own, *refs):
    (gain1, bias1, qkv_b, out_b, gain2, bias2, up_b, down_b, tab,
     y_out, x_grad, wide_out, down_out, small_out,
     wide_own, wide_w, down_w, wide_g, down_g) = refs[:19]
    wide_parts, down_parts = refs[19:24], refs[24:29]
    (small_own, small, small_grads, small_bufs, small_grad_bufs,
     n1, n2, qkv, probs, ctx, slope, act, d_qkv, hidden1, d_hidden1, send_sems, recv_sems) = refs[29:]
    saved = (n1, n2, qkv, probs, ctx, slope, act, d_qkv)
    weights, grads = (wide_w, down_w), (wide_g, down_g)
    pos = positions()
    rank = pos[0] * 8 + pos[1]
    wide_own[:, :, :OUT] = qkv_own[...]
    wide_own[:, :, OUT:UP] = out_own[...]
    wide_own[:, :, UP:] = up_own[...]
    place_small(rank, (gain1, bias1, qkv_b, out_b, gain2, bias2, up_b, down_b), small_own)
    small_grads[...] = jnp.zeros_like(small_grads)
    entry_barrier(pos)
    copies = Copies(send_sems, recv_sems)

    small_gen = small_reduce_steps(copies, pos, small_own, small_bufs, small)
    done = []
    pieces = []
    for i in range(LAYERS):
        pieces.append(gather_steps(copies, pos, wide_own.at[i], wide_w.at[i], 0, UP))
        pieces.append(gather_steps(copies, pos, wide_own.at[i], wide_w.at[i], UP, UP))
        pieces.append(gather_steps(copies, pos, down_own.at[i], down_w.at[i], 0, WIDE))
    gather = gather_program(pieces, (0, 1, 6, 14, 22, 31), small_gen, done)

    def gather_until(piece):
        while piece not in done:
            next(gather)

    def gather_pump(count):
        for _ in range(count):
            next(gather, None)

    gather_until(0)

    def forward_hooks(layer):
        def hooks(name):
            if name == 'out':
                gather_until(3 * layer + 1)
            elif name == 'up':
                gather_until(3 * layer + 2)
            else:
                gather_pump(2)
        return hooks

    hidden1[...] = layer_forward(0, x, weights, small, tab, saved, forward_hooks(0))
    gather_until(3)
    y_out[...] = layer_forward(1, hidden1, weights, small, tab, saved, forward_hooks(1))
    gather_until(5)

    queue = ScatterQueue()

    def add(layer, kind, lo):
        parts = (wide_parts, down_parts)[kind]
        out = (wide_out, down_out)[kind]
        queue.add(scatter_chunk_steps(copies, pos, grads[kind], *(ref.at[layer] for ref in parts), out.at[layer],
                                      lo, (2 * WIDE, WIDE // 2)[kind]))

    def hooks_from(layer, plan):
        calls = iter(plan)

        def hooks(name, chunk=None):
            wanted, stages = next(calls)
            assert name == wanted
            if chunk is not None:
                add(layer, *chunk)
            queue.pump(*stages)
        return hooks

    backward1 = [('down', ()), ('down', (0,)), ('up', (0,)), ('up', (0,)), ('dctx', (0,)), ('dattn', ()), ('dattn', (1,)),
                 ('dqkv', ()), ('dqkv', (0,))]
    again0 = [('norm', (0,)), ('qkv', ()), ('attn', ()), ('attn', ()), ('out', (1,)), ('up', ()),
              ('mlp', ()), ('mlp', ()), ('mlp', ()), ('mlp', (1,))]
    backward0 = [('down', ()), ('down', (0, 2)), ('up', (0, 1)), ('up', (0, 2)), ('dctx', (0, 1)), ('dattn', (2,)),
                 ('dattn', (1, 3)), ('dqkv', ()), ('dqkv', (0,))]
    d_hidden1[...] = layer_backward(1, hidden1, y_cot, weights, small, tab, saved, grads, small_grads,
                                    hooks_from(1, backward1))
    layer_forward(0, x, weights, small, tab, saved, hooks_from(0, again0))
    x_grad[...] = layer_backward(0, x, d_hidden1, weights, small, tab, saved, grads, small_grads,
                                 hooks_from(0, backward0))
    small_gen = small_reduce_steps(copies, pos, small_grads, small_grad_bufs, small_out)
    queue.drain(2, small_gen)
    for _ in small_gen:
        pass
    copies.finish()


def part_scratch(rows, width):
    return [pltpu.VMEM((LAYERS, 4, 2, 2, rows, width), jnp.float32),
            pltpu.VMEM((LAYERS, 4, 2, rows, width // 2), jnp.float32),
            pltpu.VMEM((LAYERS, 4, 2, rows, width // 2), jnp.float32),
            pltpu.VMEM((LAYERS, 4, rows, width), jnp.float32),
            pltpu.VMEM((LAYERS, 3, rows, width), jnp.float32)]


def step_call(x, y_cot, matrices, vectors, tab):
    tokens, d_model = x.shape
    rows, down_rows = matrices[1].shape[1], matrices[3].shape[1]
    vmem = pl.BlockSpec(memory_space=pltpu.VMEM)
    bf16, f32 = jnp.bfloat16, jnp.float32
    small = (LAYERS * SMALL, d_model)
    n_sems = 6 * 2 + 6 * 23 + 8 * 12
    return pl.pallas_call(
        step_kernel,
        out_shape=(jax.ShapeDtypeStruct(x.shape, bf16), jax.ShapeDtypeStruct(x.shape, bf16),
                   jax.ShapeDtypeStruct((LAYERS, rows, ACOLS), bf16),
                   jax.ShapeDtypeStruct((LAYERS, down_rows, d_model), bf16), jax.ShapeDtypeStruct(small, f32)),
        in_specs=[vmem] * (2 + 4 + 8 + 1), out_specs=(vmem,) * 5,
        scratch_shapes=[
            pltpu.VMEM((LAYERS, rows, ACOLS), bf16),
            pltpu.VMEM((LAYERS, 4, 2, 2, 2, rows, ACOLS), bf16),
            pltpu.VMEM((LAYERS, 4, 2, 2, 2, down_rows, d_model), bf16),
            pltpu.VMEM((4, 2, 2, 2, rows, ACOLS), f32),
            pltpu.VMEM((4, 2, 2, 2, down_rows, d_model), f32),
            *part_scratch(rows, ACOLS), *part_scratch(down_rows, d_model),
            pltpu.VMEM(small, f32),
            pltpu.VMEM(small, f32),
            pltpu.VMEM(small, f32),
            pltpu.VMEM((9,) + small, f32),
            pltpu.VMEM((9,) + small, f32),
            pltpu.VMEM((tokens, d_model), bf16),
            pltpu.VMEM((tokens, d_model), bf16),
            pltpu.VMEM((3, tokens, d_model), bf16),
            pltpu.VMEM((tokens // SEQ, 4, 2, SEQ, SEQ), f32),
            pltpu.VMEM((tokens, d_model), bf16),
            pltpu.VMEM((tokens, 4 * d_model), f32),
            pltpu.VMEM((tokens, 4 * d_model), bf16),
            pltpu.VMEM((tokens, 3 * d_model), bf16),
            pltpu.VMEM((tokens, d_model), bf16),
            pltpu.VMEM((tokens, d_model), bf16),
            pltpu.SemaphoreType.DMA((n_sems,)), pltpu.SemaphoreType.DMA((n_sems,))],
        compiler_params=pltpu.CompilerParams(collective_id=0, has_side_effects=True,
                                             vmem_limit_bytes=67043328),
    )(x, y_cot, *matrices, *vectors, tab)


def finish_kernel(y_in, x_grad_in, wide, down, small, y_out, x_grad, gain1, bias1, qkv_g, qkv_b, out_g, out_b,
                  gain2, bias2, up_g, up_b, down_g, down_b):
    y_out[...] = y_in[...]
    x_grad[...] = x_grad_in[...]
    qkv_g[...] = wide[:, :, :OUT]
    out_g[...] = wide[:, :, OUT:UP]
    up_g[...] = wide[:, :, UP:]
    down_g[...] = down[...]
    rank = lax.axis_index('node') * 8 + lax.axis_index('local')
    for ref, (row, count) in zip((gain1, bias1, qkv_b, out_b, gain2, bias2, up_b, down_b), VECTOR_ROWS):
        sums = []
        for layer in range(LAYERS):
            lines = [small[pl.ds(layer * SMALL + row + i, 1), :] for i in range(count)]
            sums.append(jnp.concatenate(lines, axis=1))
        sums = jnp.concatenate(sums, axis=0).astype(jnp.bfloat16)
        ref[...] = dot_bt(sums, places(rank, ref.shape[1], count * WIDE)).astype(jnp.bfloat16)


def finish_call(y, x_grad, wide, down, small, shapes):
    vmem = pl.BlockSpec(memory_space=pltpu.VMEM)
    return pl.pallas_call(
        finish_kernel, out_shape=tuple(jax.ShapeDtypeStruct(s, jnp.bfloat16) for s in shapes),
        in_specs=[vmem] * 5, out_specs=(vmem,) * len(shapes),
    )(y, x_grad, wide, down, small)


def rope_table(seq_len, rot_dim):
    inv_freq = 1.0 / (np.float32(10000.0) ** (np.arange(0, rot_dim, 2, dtype=np.float32) / np.float32(rot_dim)))
    angles = np.arange(seq_len, dtype=np.float32)[:, None] * inv_freq[None, :].astype(np.float32)
    cos, sin = np.cos(angles), np.sin(angles)
    none = np.zeros_like(sin)
    rest = np.zeros((seq_len, 3 * rot_dim), np.float32)
    parts = ([cos, cos, rest + 1.0], [-sin, none, rest], [none, sin, rest])
    return np.stack([np.tile(np.concatenate(p, axis=-1), (1, 2)) for p in parts]).astype(np.float32)


def solution(mesh):
    shard_axes = ('node', 'local')
    act_spec = P(shard_axes)
    param_spec = P(None, shard_axes)

    def device_step(x, y_cot, ln1_gain, ln1_bias, qkv_weight, qkv_bias, out_weight, out_bias,
                    ln2_gain, ln2_bias, up_weight, up_bias, down_weight, down_bias):
        d_model, rows = x.shape[2], out_weight.shape[1]
        flat = (x.shape[0] * x.shape[1], d_model)
        qkv_flat = (LAYERS, rows, 3 * d_model)
        matrices = (qkv_weight.reshape(qkv_flat), out_weight, up_weight, down_weight)
        vectors = (ln1_gain, ln1_bias, qkv_bias, out_bias, ln2_gain, ln2_bias, up_bias, down_bias)
        sums = step_call(x.reshape(flat), y_cot.reshape(flat), matrices, vectors, rope_table(x.shape[1], qkv_weight.shape[3] // 12))
        shapes = [flat, flat, ln1_gain.shape, ln1_bias.shape, qkv_flat, qkv_bias.shape, out_weight.shape, out_bias.shape,
                  ln2_gain.shape, ln2_bias.shape, up_weight.shape, up_bias.shape, down_weight.shape, down_bias.shape]
        outs = list(finish_call(*sums, shapes))
        outs[0], outs[1], outs[4] = outs[0].reshape(x.shape), outs[1].reshape(x.shape), outs[4].reshape(qkv_weight.shape)
        return tuple(outs)

    return jax.shard_map(device_step, mesh=mesh,
                         in_specs=(act_spec, act_spec) + (param_spec,) * 12,
                         out_specs=(act_spec, act_spec) + (param_spec,) * 12,
                         check_vma=False)
```

profile of v0, /device:TPU:0, one launch (start us, length us, event | category | flops | bytes accessed | tf_op | source)
XLA Modules:
  0.0 226.9 jit_solution(15934522293785851474)
XLA Ops:
  0.6 1.7 reshape.48.qkv_own
  2.3 220.5 %shard_map.254 = (bf16[256,512]{1,0:T(8,128)(2,1)}, bf16[256,512]{1,0:T(8,128)(2,1)}, bf16[2,16,4096]{2,1,0:T(8,128)(2,1)}, bf16[2,64,512]{2,1,0:T(8,128)(2,1)}, f32[32,512]{1,0:T(8,128)}) custom-call(bf16[256,512]{1,0:T(8,128)(2,1)} %bitcast.6, bf16[256,512]{1,0:T(8,128)(2,1)} %bitcast.7, bf16[2,16,1536]{2,1,0:T(8,128)(2,1)} %reshape.48.qkv_own, ...), custom_call_target="tpu_custom_call" | custom-call | tf_op jit(solution)/shard_map/pallas_call | solution.py:545
  222.9 2.3 %shard_map.255 = (bf16[256,512]{1,0:T(8,128)(2,1)}, bf16[256,512]{1,0:T(8,128)(2,1)}, bf16[2,16]{1,0:T(2,128)(2,1)}, bf16[2,16]{1,0:T(2,128)(2,1)}, bf16[2,16,15...) custom-call(bf16[256,512]{1,0:T(8,128)(2,1)} %get-tuple-element.33.y, ...), custom_call_target="tpu_custom_call" | custom-call | tf_op jit(solution)/shard_map/pallas_call | solution.py:599
  225.2 1.7 reshape.51
where the time goes:
time: 227 us
  Pallas kernels  223 us (98%)
  local copies, waits for them, and re-layouts  3.41 us (2%)
    pallas_call x1, Pallas kernels, step_call(): pl.pallas_call(step_kernel, out_shape=(jax.ShapeDtypeStruct(x.shape, bf16...  221 us

commit v1 on v0

--- a/solution.py
+++ b/solution.py
@@ -140,19 +140,65 @@
     yield
 
 
-STEP_TIMES = (0, 4, 4.5, 8, 8.5, 12, 13, 16, 19, 22)
-
-
-def gather_program(pieces, starts, small_gen, done):
-    events = [(start + time, i, step) for i, start in enumerate(starts) for step, time in enumerate(STEP_TIMES)]
-    events += [(time, -1, step) for step, time in enumerate((0.5, 3, 6, 8, 11))]
-    for _, i, step in sorted(events):
-        if i < 0:
+def gather_plane_first_steps(copies, pos, own, full, lo, width):
+    z, l, c, x, y, partner, x_nbr, y_nbr, z_others = pos
+    half = width // 2
+    cols, cols_a, cols_b = pl.ds(lo, width), pl.ds(lo, half), pl.ds(lo + half, half)
+    after = ((z + 1) % 4, l)
+    z_order = [z, (z + 3) % 4, (z + 2) % 4, (z + 1) % 4]
+    mine, own_cols = full.at[z, y, x, c, :, cols], own.at[:, cols]
+    from_x = copies.start(own_cols, mine, x_nbr)
+    from_y = copies.start(own_cols, mine, y_nbr)
+    full[z, y, x, c, :, cols] = own[:, cols]
+    yield
+    from_x.wait_recv()
+    got = full.at[z, y, 1 - x, c, :, cols_a]
+    diag_y = copies.start(got, got, y_nbr)
+    from_y.wait_recv()
+    got = full.at[z, 1 - y, x, c, :, cols_b]
+    diag_x = copies.start(got, got, x_nbr)
+    yield
+    diag_y.wait_recv()
+    diag_x.wait_recv()
+    to_partner = []
+    for k in range(4):
+        got = full.at[z_order[k], :, :, c, :, cols]
+        if k < 3:
+            from_z = copies.start(got, got, after)
+        to_partner.append(copies.start(got, got, partner))
+        yield
+        if k < 3:
+            from_z.wait_recv()
+    for copy in to_partner:
+        copy.wait_recv()
+    yield
+
+
+GATHER_ORDER = 'afcbacbafcadcbfeaabccdaafbbeccdbbdaecaeddfcbeebddeeddefef'
+SMALL_TURNS = (3, 6, 10, 14, 18)
+GATHER_PUMPS = ('21211015', '11452044')
+SCATTER_ORDER = 'abcabdcbaedcfedagfebhfcighdajiheagkjiflkjgmlkhmlimjgkglm'
+SCATTER_PUMPS = ('0402111100', '1040010444', '0202432104')
+
+
+def turns(letters):
+    return [ord(letter) - ord('a') for letter in letters]
+
+
+def counts_of(digits):
+    return iter([int(digit) for digit in digits])
+
+
+def gather_program(pieces, small_gen, done):
+    order = turns(GATHER_ORDER)
+    left = [order.count(i) for i in range(len(pieces))]
+    for turn, i in enumerate(order):
+        if turn in SMALL_TURNS:
             next(small_gen)
-        else:
-            next(pieces[i])
-            if step + 1 == len(STEP_TIMES):
-                done.append(i)
+        next(pieces[i])
+        left[i] -= 1
+        if not left[i]:
+            done.append(i)
         yield
 
 
@@ -189,28 +235,67 @@
     yield
 
 
-class ScatterQueue:
+def scatter_z_first_steps(copies, pos, grads, part0, ring, plane, out, lo, width):
+    z, l, c, x, y, partner, x_nbr, y_nbr, z_others = pos
+    half = width // 2
+    cols, cols_a, cols_b = pl.ds(lo, width), pl.ds(lo, half), pl.ds(lo + half, half)
+    first_a, first_b = pl.ds(0, half), pl.ds(half, half)
+    after = ((z + 1) % 4, l)
+    z_order = [z, (z + 3) % 4, (z + 2) % 4, (z + 1) % 4]
+    swap = copies.make(grads.at[:, :, :, 1 - c, :, cols], part0.at[:, :, :, :, cols], partner)
+    swap.start()
+    yield
+    swap.wait()
+    part0[:, :, :, :, cols] = part0[:, :, :, :, cols] + grads[:, :, :, c, :, cols]
+    send = copies.start(part0.at[z_order[1], :, :, :, cols], ring.at[0], after)
+    yield
+    for k in (1, 2):
+        send.wait_recv()
+        ring[k - 1] = ring[k - 1] + part0[z_order[k + 1], :, :, :, cols]
+        send = copies.start(ring.at[k - 1], ring.at[k], after)
+        yield
+    send.wait_recv()
+    ring[2] = ring[2] + part0[z, :, :, :, cols]
+    send_a = copies.start(ring.at[2, :, 1 - x, :, first_a], plane.at[:2, :, first_a], x_nbr)
+    send_b = copies.start(ring.at[2, 1 - y, :, :, first_b], plane.at[:2, :, first_b], y_nbr)
+    yield
+    send_a.wait_recv()
+    plane[:2, :, first_a] = plane[:2, :, first_a] + ring[2, :, x, :, first_a]
+    send_a = copies.start(plane.at[1 - y, :, first_a], plane.at[2, :, first_a], y_nbr)
+    send_b.wait_recv()
+    plane[:2, :, first_b] = plane[:2, :, first_b] + ring[2, y, :, :, first_b]
+    send_b = copies.start(plane.at[1 - x, :, first_b], plane.at[2, :, first_b], x_nbr)
+    yield
+    send_a.wait_recv()
+    send_b.wait_recv()
+    out[:, cols_a] = (plane[y, :, first_a] + plane[2, :, first_a]).astype(out.dtype)
+    out[:, cols_b] = (plane[x, :, first_b] + plane[2, :, first_b]).astype(out.dtype)
+    yield
+
+
+class ScatterProgram:
     def __init__(self):
-        self.waiting = [[], [], [], []]
+        self.chunks, self.turn, self.order = [], 0, turns(SCATTER_ORDER)
 
     def add(self, chunk):
         next(chunk)
-        self.waiting[0].append(chunk)
-
-    def pump(self, *stages):
-        for stage in stages:
-            if self.waiting[stage]:
-                chunk = self.waiting[stage].pop(0)
-                next(chunk)
-                if stage < 3:
-                    self.waiting[stage + 1].append(chunk)
-
-    def drain(self, lag, between):
-        while any(self.waiting):
+        self.chunks.append(chunk)
+
+    def pump(self, count):
+        while count and self.turn < len(self.order) and self.order[self.turn] < len(self.chunks):
+            next(self.chunks[self.order[self.turn]])
+            self.turn += 1
+            count -= 1
+
+    def ensure(self, idx):
+        while idx not in self.order[:self.turn]:
+            assert self.order[self.turn] < len(self.chunks)
+            self.pump(1)
+
+    def finish(self, between):
+        while self.turn < len(self.order):
             next(between, None)
-            for stage in range(4):
-                if len(self.waiting[stage]) >= lag or not any(self.waiting[:stage]):
-                    self.pump(stage)
+            self.pump(1)
 
 
 def dot(first, second):
@@ -350,11 +435,14 @@
     put_small(5, d_out32)
     half = WIDE // 2
     for k in range(2):
+        hooks.free(k)
         value = dot_at(act[...], d_out[:, k * half:(k + 1) * half])
         down_g[:, :, :, :, :, k * half:(k + 1) * half] = value.reshape(down_g.shape[:5] + (half,))
         hooks('down', (1, k * half))
     d_n2 = None
     for k in range(4):
+        if k % 2 == 0:
+            hooks.free(2 + k // 2)
         d_act = dot_bt(d_out[...], down_weight_part(down_w, layer, k)).astype(jnp.bfloat16)
         d_pre = d_act.astype(jnp.float32) * slope[:, k * WIDE:(k + 1) * WIDE]
         put_small(6 + k, d_pre)
@@ -366,6 +454,7 @@
         if k % 2:
             hooks('up', (0, UP + (k - 1) * WIDE))
     d_n2 = d_n2.astype(jnp.bfloat16)
+    hooks.free(4)
     put(OUT, dot_at(ctx[...], d_out[...]))
     ctx[...] = dot_bt(d_out[...], weight(wide_w, layer, OUT)).astype(jnp.bfloat16)
     hooks('dctx')
@@ -401,12 +490,13 @@
             d_qkv[:, lo:lo + PAIR] = part.astype(jnp.bfloat16)
     d_n1 = None
     for t in (2, 1, 0):
+        if t == 1:
+            hooks.free(5)
         piece = d_qkv[:, t * WIDE:(t + 1) * WIDE]
         put(t * WIDE, dot_at(n1[...], piece))
         term = dot_bt(piece, weight(wide_w, layer, t * WIDE))
         d_n1 = term if d_n1 is None else d_n1 + term
-        if t != 1:
-            hooks('dqkv', (0, (t // 2) * 2 * WIDE))
+        hooks('dqkv', (0, t * WIDE))
     d_n1 = d_n1.astype(jnp.bfloat16).astype(jnp.float32)
     d_n2 = d_n2.astype(jnp.float32)
     scaled, rstd = normalised(hidden[...].astype(jnp.float32))
@@ -442,8 +532,9 @@
      y_out, x_grad, wide_out, down_out, small_out,
      wide_own, wide_w, down_w, wide_g, down_g) = refs[:19]
     wide_parts, down_parts = refs[19:24], refs[24:29]
+    ring, plane = refs[29:31]
     (small_own, small, small_grads, small_bufs, small_grad_bufs,
-     n1, n2, qkv, probs, ctx, slope, act, d_qkv, hidden1, d_hidden1, send_sems, recv_sems) = refs[29:]
+     n1, n2, qkv, probs, ctx, slope, act, d_qkv, hidden1, d_hidden1, send_sems, recv_sems) = refs[31:]
     saved = (n1, n2, qkv, probs, ctx, slope, act, d_qkv)
     weights, grads = (wide_w, down_w), (wide_g, down_g)
     pos = positions()
@@ -462,8 +553,9 @@
     for i in range(LAYERS):
         pieces.append(gather_steps(copies, pos, wide_own.at[i], wide_w.at[i], 0, UP))
         pieces.append(gather_steps(copies, pos, wide_own.at[i], wide_w.at[i], UP, UP))
-        pieces.append(gather_steps(copies, pos, down_own.at[i], down_w.at[i], 0, WIDE))
-    gather = gather_program(pieces, (0, 1, 6, 14, 22, 31), small_gen, done)
+        steps = gather_plane_first_steps if i else gather_steps
+        pieces.append(steps(copies, pos, down_own.at[i], down_w.at[i], 0, WIDE))
+    gather = gather_program(pieces, small_gen, done)
 
     def gather_until(piece):
         while piece not in done:
@@ -476,13 +568,15 @@
     gather_until(0)
 
     def forward_hooks(layer):
+        counts = counts_of(GATHER_PUMPS[layer])
+
         def hooks(name):
             if name == 'out':
                 gather_until(3 * layer + 1)
             elif name == 'up':
                 gather_until(3 * layer + 2)
             else:
-                gather_pump(2)
+                gather_pump(next(counts))
         return hooks
 
     hidden1[...] = layer_forward(0, x, weights, small, tab, saved, forward_hooks(0))
@@ -490,38 +584,39 @@
     y_out[...] = layer_forward(1, hidden1, weights, small, tab, saved, forward_hooks(1))
     gather_until(5)
 
-    queue = ScatterQueue()
+    program = ScatterProgram()
 
     def add(layer, kind, lo):
-        parts = (wide_parts, down_parts)[kind]
-        out = (wide_out, down_out)[kind]
-        queue.add(scatter_chunk_steps(copies, pos, grads[kind], *(ref.at[layer] for ref in parts), out.at[layer],
-                                      lo, (2 * WIDE, WIDE // 2)[kind]))
-
-    def hooks_from(layer, plan):
-        calls = iter(plan)
-
-        def hooks(name, chunk=None):
-            wanted, stages = next(calls)
-            assert name == wanted
-            if chunk is not None:
-                add(layer, *chunk)
-            queue.pump(*stages)
-        return hooks
-
-    backward1 = [('down', ()), ('down', (0,)), ('up', (0,)), ('up', (0,)), ('dctx', (0,)), ('dattn', ()), ('dattn', (1,)),
-                 ('dqkv', ()), ('dqkv', (0,))]
-    again0 = [('norm', (0,)), ('qkv', ()), ('attn', ()), ('attn', ()), ('out', (1,)), ('up', ()),
-              ('mlp', ()), ('mlp', ()), ('mlp', ()), ('mlp', (1,))]
-    backward0 = [('down', ()), ('down', (0, 2)), ('up', (0, 1)), ('up', (0, 2)), ('dctx', (0, 1)), ('dattn', (2,)),
-                 ('dattn', (1, 3)), ('dqkv', ()), ('dqkv', (0,))]
+        if kind and lo == 0:
+            steps = scatter_z_first_steps(copies, pos, down_g, down_parts[0].at[layer], ring.at[layer], plane.at[layer],
+                                          down_out.at[layer], lo, WIDE // 2)
+        else:
+            width = WIDE // 2 if kind else WIDE if layer == 0 and lo < 2 * WIDE else 2 * WIDE
+            parts = (wide_parts, down_parts)[kind]
+            steps = scatter_chunk_steps(copies, pos, grads[kind], *(ref.at[layer] for ref in parts),
+                                        (wide_out, down_out)[kind].at[layer], lo, width)
+        program.add(steps)
+
+    class Hooks:
+        def __init__(self, layer, counts, reused):
+            self.layer, self.counts, self.reused = layer, counts_of(counts), reused
+
+        def free(self, idx):
+            if self.reused:
+                program.ensure(idx)
+
+        def __call__(self, name, chunk=None):
+            if chunk is not None and (self.layer == 0 or chunk != (0, WIDE)):
+                add(self.layer, *chunk)
+            program.pump(next(self.counts))
+
     d_hidden1[...] = layer_backward(1, hidden1, y_cot, weights, small, tab, saved, grads, small_grads,
-                                    hooks_from(1, backward1))
-    layer_forward(0, x, weights, small, tab, saved, hooks_from(0, again0))
+                                    Hooks(1, SCATTER_PUMPS[0], False))
+    layer_forward(0, x, weights, small, tab, saved, Hooks(0, SCATTER_PUMPS[1], False))
     x_grad[...] = layer_backward(0, x, d_hidden1, weights, small, tab, saved, grads, small_grads,
-                                 hooks_from(0, backward0))
+                                 Hooks(0, SCATTER_PUMPS[2], True))
     small_gen = small_reduce_steps(copies, pos, small_grads, small_grad_bufs, small_out)
-    queue.drain(2, small_gen)
+    program.finish(small_gen)
     for _ in small_gen:
         pass
     copies.finish()
@@ -541,7 +636,7 @@
     vmem = pl.BlockSpec(memory_space=pltpu.VMEM)
     bf16, f32 = jnp.bfloat16, jnp.float32
     small = (LAYERS * SMALL, d_model)
-    n_sems = 6 * 2 + 6 * 23 + 8 * 12
+    n_sems = 6 * 2 + 6 * 23 + 8 * 13
     return pl.pallas_call(
         step_kernel,
         out_shape=(jax.ShapeDtypeStruct(x.shape, bf16), jax.ShapeDtypeStruct(x.shape, bf16),
@@ -555,6 +650,8 @@
             pltpu.VMEM((4, 2, 2, 2, rows, ACOLS), f32),
             pltpu.VMEM((4, 2, 2, 2, down_rows, d_model), f32),
             *part_scratch(rows, ACOLS), *part_scratch(down_rows, d_model),
+            pltpu.VMEM((LAYERS, 3, 2, 2, down_rows, d_model // 2), f32),
+            pltpu.VMEM((LAYERS, 3, down_rows, d_model // 2), f32),
             pltpu.VMEM(small, f32),
             pltpu.VMEM(small, f32),
             pltpu.VMEM(small, f32),

time: 227 us -> 209 us (0.921)
  Pallas kernels: 223 us -> 205 us
    pallas_call x1, Pallas kernels: 221 us -> 202 us  [step_call(): pl.pallas_call(step_kernel, out_shape=(jax.ShapeDtypeStruct(x.shape, bf16...]
where the time goes in v1:
time: 209 us
  Pallas kernels  205 us (98%)
  local copies, waits for them, and re-layouts  3.41 us (2%)
    pallas_call x1, Pallas kernels, step_call(): pl.pallas_call(step_kernel, out_shape=(jax.ShapeDtypeStruct(x.shape, bf16...  202 us

profile of v1, /device:TPU:0, one launch (start us, length us, event | category | flops | bytes accessed | tf_op | source)
XLA Modules:
  0.0 208.8 jit_solution(921732854911166405)
XLA Ops:
  0.6 1.7 reshape.48.qkv_own
  2.3 202.4 %shard_map.254 = (bf16[256,512]{1,0:T(8,128)(2,1)}, bf16[256,512]{1,0:T(8,128)(2,1)}, bf16[2,16,4096]{2,1,0:T(8,128)(2,1)}, bf16[2,64,512]{2,1,0:T(8,128)(2,1)}, f32[32,512]{1,0:T(8,128)}) custom-call(bf16[256,512]{1,0:T(8,128)(2,1)} %bitcast.6, bf16[256,512]{1,0:T(8,128)(2,1)} %bitcast.7, bf16[2,16,1536]{2,1,0:T(8,128)(2,1)} %reshape.48.qkv_own, ...), custom_call_target="tpu_custom_call" | custom-call | tf_op jit(solution)/shard_map/pallas_call | solution.py:640
  204.8 2.3 %shard_map.255 = (bf16[256,512]{1,0:T(8,128)(2,1)}, bf16[256,512]{1,0:T(8,128)(2,1)}, bf16[2,16]{1,0:T(2,128)(2,1)}, bf16[2,16]{1,0:T(2,128)(2,1)}, bf16[2,16,15...) custom-call(bf16[256,512]{1,0:T(8,128)(2,1)} %get-tuple-element.33.y, ...), custom_call_target="tpu_custom_call" | custom-call | tf_op jit(solution)/shard_map/pallas_call | solution.py:696
  207.1 1.7 reshape.51

commit v2 on v1

--- a/solution.py
+++ b/solution.py
@@ -12,6 +12,10 @@
 LAYERS = 2
 ROWS = 16
 SMALL = 16
+WIDE = 512
+PAIR = 128
+SEQ = 128
+OUT, UP, ACOLS = 3 * WIDE, 4 * WIDE, 8 * WIDE
 
 
 def positions():
@@ -27,6 +31,10 @@
     return z, l, c, x, y, partner, x_nbr, y_nbr, z_others
 
 
+def ring_of(z, l):
+    return ((z + 1) % 4, l), [z, (z + 3) % 4, (z + 2) % 4, (z + 1) % 4]
+
+
 def entry_barrier(pos):
     z, l, c, x, y, partner, x_nbr, y_nbr, z_others = pos
     barrier = pltpu.get_barrier_semaphore()
@@ -79,8 +87,7 @@
     z, l, c, x, y, partner, x_nbr, y_nbr, z_others = pos
     half = width // 2
     cols, cols_a, cols_b = pl.ds(lo, width), pl.ds(lo, half), pl.ds(lo + half, half)
-    after = ((z + 1) % 4, l)
-    z_order = [z, (z + 3) % 4, (z + 2) % 4, (z + 1) % 4]
+    after, z_order = ring_of(z, l)
 
     def block(zz, yy, xx, cc):
         return full.at[zz, yy, xx, cc, :, cols]
@@ -144,8 +151,7 @@
     z, l, c, x, y, partner, x_nbr, y_nbr, z_others = pos
     half = width // 2
     cols, cols_a, cols_b = pl.ds(lo, width), pl.ds(lo, half), pl.ds(lo + half, half)
-    after = ((z + 1) % 4, l)
-    z_order = [z, (z + 3) % 4, (z + 2) % 4, (z + 1) % 4]
+    after, z_order = ring_of(z, l)
     mine, own_cols = full.at[z, y, x, c, :, cols], own.at[:, cols]
     from_x = copies.start(own_cols, mine, x_nbr)
     from_y = copies.start(own_cols, mine, y_nbr)
@@ -174,11 +180,12 @@
     yield
 
 
-GATHER_ORDER = 'afcbacbafcadcbfeaabccdaafbbeccdbbdaecaeddfcbeebddeeddefef'
+GATHER_ORDER = 'acfbacfbdeaaacccfbbbdeacaafccbacabbdddceeebbfdeddeededfef'
 SMALL_TURNS = (3, 6, 10, 14, 18)
-GATHER_PUMPS = ('21211015', '11452044')
-SCATTER_ORDER = 'abcabdcbaedcfedagfebhfcighdajiheagkjiflkjgmlkhmlimjgkglm'
-SCATTER_PUMPS = ('0402111100', '1040010444', '0202432104')
+GATHER_PUMPS = ('14400305', '01100503')
+SCATTER_ORDERS = ('abcabdcbaedcbfedacgfebdahgfcaeigdfjhiegkjifhlkjgibmlkhjcnmli', 'khdomjhlenkmfonlgominjoklm')
+SCATTER_PUMPS = ('0304101110', '0012002313', '0124432324')
+DIRECT = (0, WIDE)
 
 
 def turns(letters):
@@ -202,10 +209,11 @@
         yield
 
 
-def scatter_chunk_steps(copies, pos, grads, part0, partx, party, last, partz, out, lo, width):
+def scatter_chunk_steps(copies, pos, grads, part0, partx, party, last, partz, out, lo, width, direct):
     z, l, c, x, y, partner, x_nbr, y_nbr, z_others = pos
     half = width // 2
     cols, cols_a, cols_b = pl.ds(lo, width), pl.ds(lo, half), pl.ds(lo + half, half)
+    after, z_order = ring_of(z, l)
     hcols = pl.ds(lo // 2, half)
     swap = copies.make(grads.at[:, :, :, 1 - c, :, cols], part0.at[:, :, :, :, cols], partner)
     swap.start()
@@ -226,11 +234,22 @@
     send_b.wait_recv()
     last[:, :, cols_a] = last[:, :, cols_a] + partx[:, y, :, hcols]
     last[:, :, cols_b] = last[:, :, cols_b] + party[:, x, :, hcols]
-    sends = [copies.start(last.at[zo, :, cols], partz.at[k, :, cols], (zo, l)) for k, zo in enumerate(z_others)]
-    yield
-    for copy in sends:
-        copy.wait_recv()
-    total = (last[z, :, cols] + partz[0, :, cols]) + (partz[1, :, cols] + partz[2, :, cols])
+    if direct:
+        sends = [copies.start(last.at[zo, :, cols], partz.at[k, :, cols], (zo, l)) for k, zo in enumerate(z_others)]
+        yield
+        for copy in sends:
+            copy.wait_recv()
+        total = (last[z, :, cols] + partz[0, :, cols]) + (partz[1, :, cols] + partz[2, :, cols])
+    else:
+        send = copies.start(last.at[z_order[1], :, cols], partz.at[0, :, cols], after)
+        yield
+        for k in (1, 2):
+            send.wait_recv()
+            partz[k - 1, :, cols] = partz[k - 1, :, cols] + last[z_order[k + 1], :, cols]
+            send = copies.start(partz.at[k - 1, :, cols], partz.at[k, :, cols], after)
+            yield
+        send.wait_recv()
+        total = partz[2, :, cols] + last[z, :, cols]
     out[:, cols] = total.astype(out.dtype)
     yield
 
@@ -240,8 +259,7 @@
     half = width // 2
     cols, cols_a, cols_b = pl.ds(lo, width), pl.ds(lo, half), pl.ds(lo + half, half)
     first_a, first_b = pl.ds(0, half), pl.ds(half, half)
-    after = ((z + 1) % 4, l)
-    z_order = [z, (z + 3) % 4, (z + 2) % 4, (z + 1) % 4]
+    after, z_order = ring_of(z, l)
     swap = copies.make(grads.at[:, :, :, 1 - c, :, cols], part0.at[:, :, :, :, cols], partner)
     swap.start()
     yield
@@ -275,7 +293,7 @@
 
 class ScatterProgram:
     def __init__(self):
-        self.chunks, self.turn, self.order = [], 0, turns(SCATTER_ORDER)
+        self.chunks, self.turn, self.order = [], 0, [chunk for part in SCATTER_ORDERS for chunk in turns(part)]
 
     def add(self, chunk):
         next(chunk)
@@ -308,12 +326,6 @@
 
 def dot_at(first, second):
     return lax.dot_general(first, second, (((0,), (0,)), ((), ())), preferred_element_type=jnp.float32)
-
-
-WIDE = 512
-PAIR = 128
-SEQ = 128
-OUT, UP, ACOLS = 3 * WIDE, 4 * WIDE, 8 * WIDE
 
 
 def normalised(hidden32):
@@ -457,7 +469,7 @@
     hooks.free(4)
     put(OUT, dot_at(ctx[...], d_out[...]))
     ctx[...] = dot_bt(d_out[...], weight(wide_w, layer, OUT)).astype(jnp.bfloat16)
-    hooks('dctx')
+    hooks('dctx', (0, OUT))
     masks, low = head_masks(), low_half(SEQ)
     for s, j, rows, cols in attention_blocks(tokens):
         query, key, value = qkv[0, rows, cols], qkv[1, rows, cols], qkv[2, rows, cols]
@@ -490,8 +502,8 @@
             d_qkv[:, lo:lo + PAIR] = part.astype(jnp.bfloat16)
     d_n1 = None
     for t in (2, 1, 0):
-        if t == 1:
-            hooks.free(5)
+        if t:
+            hooks.free(7 - t)
         piece = d_qkv[:, t * WIDE:(t + 1) * WIDE]
         put(t * WIDE, dot_at(n1[...], piece))
         term = dot_bt(piece, weight(wide_w, layer, t * WIDE))
@@ -591,10 +603,10 @@
             steps = scatter_z_first_steps(copies, pos, down_g, down_parts[0].at[layer], ring.at[layer], plane.at[layer],
                                           down_out.at[layer], lo, WIDE // 2)
         else:
-            width = WIDE // 2 if kind else WIDE if layer == 0 and lo < 2 * WIDE else 2 * WIDE
+            width = WIDE // 2 if kind else WIDE if OUT <= lo < UP or (layer == 0 or lo) and lo < OUT else 2 * WIDE
             parts = (wide_parts, down_parts)[kind]
             steps = scatter_chunk_steps(copies, pos, grads[kind], *(ref.at[layer] for ref in parts),
-                                        (wide_out, down_out)[kind].at[layer], lo, width)
+                                        (wide_out, down_out)[kind].at[layer], lo, width, layer == 0 and lo in DIRECT)
         program.add(steps)
 
     class Hooks:
@@ -636,7 +648,7 @@
     vmem = pl.BlockSpec(memory_space=pltpu.VMEM)
     bf16, f32 = jnp.bfloat16, jnp.float32
     small = (LAYERS * SMALL, d_model)
-    n_sems = 6 * 2 + 6 * 23 + 8 * 13
+    n_sems = 12 + 6 * 23 + 8 * 15
     return pl.pallas_call(
         step_kernel,
         out_shape=(jax.ShapeDtypeStruct(x.shape, bf16), jax.ShapeDtypeStruct(x.shape, bf16),

time: 209 us -> 204 us (0.976)
  Pallas kernels: 205 us -> 199 us
    pallas_call x1, Pallas kernels: 202 us -> 197 us  [step_call(): pl.pallas_call(step_kernel, out_shape=(jax.ShapeDtypeStruct(x.shape, bf16...]
where the time goes in v2:
time: 204 us; the launch traced here: 203 us
  Pallas kernels  199 us (98%)
  local copies, waits for them, and re-layouts  3.41 us (2%)
    pallas_call x1, Pallas kernels, step_call(): pl.pallas_call(step_kernel, out_shape=(jax.ShapeDtypeStruct(x.shape, bf16...  197 us

profile of v2, /device:TPU:0, one launch (start us, length us, event | category | flops | bytes accessed | tf_op | source)
XLA Modules:
  0.0 203.4 jit_solution(5221805905031897523)
XLA Ops:
  0.6 1.7 reshape.48.qkv_own
  2.3 197.0 %shard_map.254 = (bf16[256,512]{1,0:T(8,128)(2,1)}, bf16[256,512]{1,0:T(8,128)(2,1)}, bf16[2,16,4096]{2,1,0:T(8,128)(2,1)}, bf16[2,64,512]{2,1,0:T(8,128)(2,1)}, f32[32,512]{1,0:T(8,128)}) custom-call(bf16[256,512]{1,0:T(8,128)(2,1)} %bitcast.6, bf16[256,512]{1,0:T(8,128)(2,1)} %bitcast.7, bf16[2,16,1536]{2,1,0:T(8,128)(2,1)} %reshape.48.qkv_own, ...), custom_call_target="tpu_custom_call" | custom-call | tf_op jit(solution)/shard_map/pallas_call | solution.py:652
  199.4 2.3 %shard_map.255 = (bf16[256,512]{1,0:T(8,128)(2,1)}, bf16[256,512]{1,0:T(8,128)(2,1)}, bf16[2,16]{1,0:T(2,128)(2,1)}, bf16[2,16]{1,0:T(2,128)(2,1)}, bf16[2,16,15...) custom-call(bf16[256,512]{1,0:T(8,128)(2,1)} %get-tuple-element.33.y, ...), custom_call_target="tpu_custom_call" | custom-call | tf_op jit(solution)/shard_map/pallas_call | solution.py:708
  201.7 1.7 reshape.51

commit v3 on v2

--- a/solution.py
+++ b/solution.py
@@ -147,49 +147,18 @@
     yield
 
 
-def gather_plane_first_steps(copies, pos, own, full, lo, width):
-    z, l, c, x, y, partner, x_nbr, y_nbr, z_others = pos
-    half = width // 2
-    cols, cols_a, cols_b = pl.ds(lo, width), pl.ds(lo, half), pl.ds(lo + half, half)
-    after, z_order = ring_of(z, l)
-    mine, own_cols = full.at[z, y, x, c, :, cols], own.at[:, cols]
-    from_x = copies.start(own_cols, mine, x_nbr)
-    from_y = copies.start(own_cols, mine, y_nbr)
-    full[z, y, x, c, :, cols] = own[:, cols]
-    yield
-    from_x.wait_recv()
-    got = full.at[z, y, 1 - x, c, :, cols_a]
-    diag_y = copies.start(got, got, y_nbr)
-    from_y.wait_recv()
-    got = full.at[z, 1 - y, x, c, :, cols_b]
-    diag_x = copies.start(got, got, x_nbr)
-    yield
-    diag_y.wait_recv()
-    diag_x.wait_recv()
-    to_partner = []
-    for k in range(4):
-        got = full.at[z_order[k], :, :, c, :, cols]
-        if k < 3:
-            from_z = copies.start(got, got, after)
-        to_partner.append(copies.start(got, got, partner))
-        yield
-        if k < 3:
-            from_z.wait_recv()
-    for copy in to_partner:
-        copy.wait_recv()
-    yield
-
-
-GATHER_ORDER = 'acfbacfbdeaaacccfbbbdeacaafccbacabbdddceeebbfdeddeededfef'
-SMALL_TURNS = (3, 6, 10, 14, 18)
-GATHER_PUMPS = ('14400305', '01100503')
-SCATTER_ORDERS = ('abcabdcbaedcbfedacgfebdahgfcaeigdfjhiegkjifhlkjgibmlkhjcnmli', 'khdomjhlenkmfonlgominjoklm')
-SCATTER_PUMPS = ('0304101110', '0012002313', '0124432324')
+GATHER_ORDERS = ('azcbdaaccefbzbaaddccbbacbzddefefaadczcbbaefefzcbaddefcbdefde', 'fefef')
+GATHER_PUMPS = ('15001211', '10205331')
+SCATTER_ORDERS = ('abcabdcbeadcfbedgacbfehdcgfiedgjfebhikgfcjilhagdkjamielknhji', 'fmzlokjgmnlkzomlinzmjohkhlnmoz')
+SCATTER_PUMPS = ('0200121000', '1401111220', '4320442144')
 DIRECT = (0, WIDE)
 
 
-def turns(letters):
-    return [ord(letter) - ord('a') for letter in letters]
+SMALL_TURN = ord('z') - ord('a')
+
+
+def turns(parts):
+    return [ord(letter) - ord('a') for part in parts for letter in part]
 
 
 def counts_of(digits):
@@ -197,11 +166,12 @@
 
 
 def gather_program(pieces, small_gen, done):
-    order = turns(GATHER_ORDER)
+    order = turns(GATHER_ORDERS)
     left = [order.count(i) for i in range(len(pieces))]
-    for turn, i in enumerate(order):
-        if turn in SMALL_TURNS:
+    for i in order:
+        if i == SMALL_TURN:
             next(small_gen)
+            continue
         next(pieces[i])
         left[i] -= 1
         if not left[i]:
@@ -293,26 +263,22 @@
 
 class ScatterProgram:
     def __init__(self):
-        self.chunks, self.turn, self.order = [], 0, [chunk for part in SCATTER_ORDERS for chunk in turns(part)]
-
-    def add(self, chunk):
+        self.chunks, self.turn = {}, 0
+        self.order = turns(SCATTER_ORDERS)
+
+    def add(self, chunk, idx=None):
         next(chunk)
-        self.chunks.append(chunk)
+        self.chunks[len(self.chunks) if idx is None else idx] = chunk
 
     def pump(self, count):
-        while count and self.turn < len(self.order) and self.order[self.turn] < len(self.chunks):
+        while count and self.turn < len(self.order) and self.order[self.turn] in self.chunks:
             next(self.chunks[self.order[self.turn]])
             self.turn += 1
             count -= 1
 
     def ensure(self, idx):
         while idx not in self.order[:self.turn]:
-            assert self.order[self.turn] < len(self.chunks)
-            self.pump(1)
-
-    def finish(self, between):
-        while self.turn < len(self.order):
-            next(between, None)
+            assert self.order[self.turn] in self.chunks
             self.pump(1)
 
 
@@ -565,8 +531,7 @@
     for i in range(LAYERS):
         pieces.append(gather_steps(copies, pos, wide_own.at[i], wide_w.at[i], 0, UP))
         pieces.append(gather_steps(copies, pos, wide_own.at[i], wide_w.at[i], UP, UP))
-        steps = gather_plane_first_steps if i else gather_steps
-        pieces.append(steps(copies, pos, down_own.at[i], down_w.at[i], 0, WIDE))
+        pieces.append(gather_steps(copies, pos, down_own.at[i], down_w.at[i], 0, WIDE))
     gather = gather_program(pieces, small_gen, done)
 
     def gather_until(piece):
@@ -627,10 +592,8 @@
     layer_forward(0, x, weights, small, tab, saved, Hooks(0, SCATTER_PUMPS[1], False))
     x_grad[...] = layer_backward(0, x, d_hidden1, weights, small, tab, saved, grads, small_grads,
                                  Hooks(0, SCATTER_PUMPS[2], True))
-    small_gen = small_reduce_steps(copies, pos, small_grads, small_grad_bufs, small_out)
-    program.finish(small_gen)
-    for _ in small_gen:
-        pass
+    program.add(small_reduce_steps(copies, pos, small_grads, small_grad_bufs, small_out), SMALL_TURN)
+    program.pump(len(program.order))
     copies.finish()
 
 

time: 204 us -> 189 us (0.926)
  Pallas kernels: 199 us -> 185 us
    pallas_call x1, Pallas kernels: 197 us -> 182 us  [step_call(): pl.pallas_call(step_kernel, out_shape=(jax.ShapeDtypeStruct(x.shape, bf16...]
where the time goes in v3:
time: 189 us
  Pallas kernels  185 us (98%)
  local copies, waits for them, and re-layouts  3.41 us (2%)
    pallas_call x1, Pallas kernels, step_call(): pl.pallas_call(step_kernel, out_shape=(jax.ShapeDtypeStruct(x.shape, bf16...  182 us

profile of v3, /device:TPU:0, one launch (start us, length us, event | category | flops | bytes accessed | tf_op | source)
XLA Modules:
  0.0 188.7 jit_solution(3138582549056545121)
XLA Ops:
  0.6 1.7 reshape.48.qkv_own
  2.3 182.3 %shard_map.254 = (bf16[256,512]{1,0:T(8,128)(2,1)}, bf16[256,512]{1,0:T(8,128)(2,1)}, bf16[2,16,4096]{2,1,0:T(8,128)(2,1)}, bf16[2,64,512]{2,1,0:T(8,128)(2,1)}, f32[32,512]{1,0:T(8,128)}) custom-call(bf16[256,512]{1,0:T(8,128)(2,1)} %bitcast.6, bf16[256,512]{1,0:T(8,128)(2,1)} %bitcast.7, bf16[2,16,1536]{2,1,0:T(8,128)(2,1)} %reshape.48.qkv_own, ...), custom_call_target="tpu_custom_call" | custom-call | tf_op jit(solution)/shard_map/pallas_call | solution.py:615
  184.7 2.3 %shard_map.255 = (bf16[256,512]{1,0:T(8,128)(2,1)}, bf16[256,512]{1,0:T(8,128)(2,1)}, bf16[2,16]{1,0:T(2,128)(2,1)}, bf16[2,16]{1,0:T(2,128)(2,1)}, bf16[2,16,15...) custom-call(bf16[256,512]{1,0:T(8,128)(2,1)} %get-tuple-element.33.y, ...), custom_call_target="tpu_custom_call" | custom-call | tf_op jit(solution)/shard_map/pallas_call | solution.py:671
  187.0 1.7 reshape.51

commit v4 on v3

--- a/solution.py
+++ b/solution.py
@@ -147,10 +147,10 @@
     yield
 
 
-GATHER_ORDERS = ('azcbdaaccefbzbaaddccbbacbzddefefaadczcbbaefefzcbaddefcbdefde', 'fefef')
-GATHER_PUMPS = ('15001211', '10205331')
-SCATTER_ORDERS = ('abcabdcbeadcfbedgacbfehdcgfiedgjfebhikgfcjilhagdkjamielknhji', 'fmzlokjgmnlkzomlinzmjohkhlnmoz')
-SCATTER_PUMPS = ('0200121000', '1401111220', '4320442144')
+GATHER_ORDERS = ('zacbdezafcbzaacdbcbazaccdbbdaaeccabbzddefaecbddcbeeffddeeffe', 'ffeff')
+GATHER_PUMPS = ('11330204', '11113410')
+SCATTER_ORDERS = ('abcabdcbeadcfbedgacbfehdcgfiedgjfehibkgfjiaclhgakjdmilkenhji', 'mlzfokjmgnlkzomlzinmhjohklnmoz')
+SCATTER_PUMPS = ('0200121000', '1401111220', '4320440343')
 DIRECT = (0, WIDE)
 
 
@@ -329,10 +329,8 @@
     return (jnp.where(first, 1.0, 0.0).astype(jnp.bfloat16), jnp.where(first, 0.0, 1.0).astype(jnp.bfloat16))
 
 
-def attention_blocks(tokens):
-    for s in range(tokens // SEQ):
-        for j in range(WIDE // PAIR):
-            yield s, j, pl.ds(s * SEQ, SEQ), pl.ds(j * PAIR, PAIR)
+def pair_block(s, j):
+    return pl.ds(s * SEQ, SEQ), pl.ds(pl.multiple_of(j * PAIR, PAIR), PAIR)
 
 
 def layer_forward(layer, hidden, weights, small, tab, saved, hooks):
@@ -364,59 +362,66 @@
     hooks('qkv')
     causal = (lax.broadcasted_iota(jnp.int32, (SEQ, SEQ), 0) >= lax.broadcasted_iota(jnp.int32, (SEQ, SEQ), 1))
     masks, low = head_masks(), low_half(SEQ)
-    for s, j, rows, cols in attention_blocks(tokens):
-        query, key, value = qkv[0, rows, cols], qkv[1, rows, cols], qkv[2, rows, cols]
-        heads = []
-        for h in range(2):
-            scores = dot_bt(query * masks[h], key) * 0.125
-            scores = jnp.where(causal, scores, -1e30)
-            attn = jnp.exp(scores - jnp.max(scores, axis=-1, keepdims=True))
-            attn = attn / jnp.sum(attn, axis=-1, keepdims=True)
-            probs[s, j, h] = attn
-            heads.append(dot(attn.astype(jnp.bfloat16), value))
-        ctx[rows, cols] = jnp.where(low, heads[0], heads[1]).astype(jnp.bfloat16)
-        if j == 3:
-            hooks('attn')
+    for s in range(tokens // SEQ):
+        @pl.loop(0, WIDE // PAIR)
+        def attend(j, s=s):
+            rows, cols = pair_block(s, j)
+            query, key, value = qkv[0, rows, cols], qkv[1, rows, cols], qkv[2, rows, cols]
+            heads = []
+            for h in range(2):
+                scores = dot_bt(query * masks[h], key) * 0.125
+                scores = jnp.where(causal, scores, -1e30)
+                attn = jnp.exp(scores - jnp.max(scores, axis=-1, keepdims=True))
+                attn = attn / jnp.sum(attn, axis=-1, keepdims=True)
+                probs[s, j, h] = attn
+                heads.append(dot(attn.astype(jnp.bfloat16), value))
+            ctx[rows, cols] = jnp.where(low, heads[0], heads[1]).astype(jnp.bfloat16)
+        hooks('attn')
     total = hidden32 + (dot(ctx[...], weight(wide_w, layer, OUT)) + vec(2))
     hooks('out')
-    mlp = None
     for k in range(4):
         pre = dot(n2[...], weight(wide_w, layer, UP + k * WIDE)) + vec(6 + k)
         bell = lax.erf(pre * 0.7071067811865476) + 1.0
         act[:, k * WIDE:(k + 1) * WIDE] = (0.5 * pre * bell).astype(jnp.bfloat16)
         slope[:, k * WIDE:(k + 1) * WIDE] = 0.5 * bell + pre * (jnp.exp(-0.5 * pre * pre) * 0.3989422804014327)
-        if k == 0:
-            hooks('up')
+    hooks('up')
+    mlp = None
+    for k in range(4):
         term = dot(act[:, k * WIDE:(k + 1) * WIDE], down_weight_part(down_w, layer, k))
         mlp = term if mlp is None else mlp + term
         hooks('mlp')
     return (total + (mlp + vec(5))).astype(jnp.bfloat16)
 
 
-def layer_backward(layer, hidden, d_out, weights, small, tab, saved, grads, small_grads, hooks):
-    n1, n2, qkv, probs, ctx, slope, act, d_qkv = saved
-    wide_w, down_w = weights
-    wide_g, down_g = grads
-    tokens = hidden.shape[0]
-
-    def vec(row):
-        return small[pl.ds(layer * SMALL + row, 1), :]
-
-    def put_small(row, value):
-        small_grads[pl.ds(layer * SMALL + row, 1), :] = jnp.sum(value, axis=0, keepdims=True)
-
-    def put(lo, value):
-        wide_g[:, :, :, :, :, lo:lo + WIDE] = value.reshape(wide_g.shape[:5] + (WIDE,))
-
-    d_out32 = d_out[...].astype(jnp.float32)
-    put_small(2, d_out32)
-    put_small(5, d_out32)
+def down_gradients(d_out, act, down_g, hooks):
     half = WIDE // 2
     for k in range(2):
         hooks.free(k)
         value = dot_at(act[...], d_out[:, k * half:(k + 1) * half])
         down_g[:, :, :, :, :, k * half:(k + 1) * half] = value.reshape(down_g.shape[:5] + (half,))
         hooks('down', (1, k * half))
+
+
+def layer_backward(layer, hidden, d_out, weights, small, tab, saved, grads, small_grads, hooks):
+    n1, n2, qkv, probs, ctx, slope, act, d_qkv = saved
+    wide_w, down_w = weights
+    wide_g, down_g = grads
+    tokens = hidden.shape[0]
+
+    def vec(row):
+        return small[pl.ds(layer * SMALL + row, 1), :]
+
+    def put_small(row, value):
+        small_grads[pl.ds(layer * SMALL + row, 1), :] = jnp.sum(value, axis=0, keepdims=True)
+
+    def put(lo, value):
+        wide_g[:, :, :, :, :, lo:lo + WIDE] = value.reshape(wide_g.shape[:5] + (WIDE,))
+
+    d_out32 = d_out[...].astype(jnp.float32)
+    put_small(2, d_out32)
+    put_small(5, d_out32)
+    if layer == 0:
+        down_gradients(d_out, act, down_g, hooks)
     d_n2 = None
     for k in range(4):
         if k % 2 == 0:
@@ -437,23 +442,25 @@
     ctx[...] = dot_bt(d_out[...], weight(wide_w, layer, OUT)).astype(jnp.bfloat16)
     hooks('dctx', (0, OUT))
     masks, low = head_masks(), low_half(SEQ)
-    for s, j, rows, cols in attention_blocks(tokens):
-        query, key, value = qkv[0, rows, cols], qkv[1, rows, cols], qkv[2, rows, cols]
-        d_ctx = ctx[rows, cols]
-        d_q, d_k, d_v = [], [], []
-        for h in range(2):
-            attn = probs[s, j, h]
-            d_probs = dot_bt(d_ctx * masks[h], value).astype(jnp.bfloat16).astype(jnp.float32)
-            d_v.append(dot_at(attn.astype(jnp.bfloat16), d_ctx))
-            inner = jnp.sum(d_probs * attn, axis=-1, keepdims=True)
-            d_scores = (attn * (d_probs - inner) * 0.125).astype(jnp.bfloat16)
-            d_q.append(dot(d_scores, key))
-            d_k.append(dot_at(d_scores, query))
-        qkv[0, rows, cols] = jnp.where(low, d_q[0], d_q[1]).astype(jnp.bfloat16)
-        qkv[1, rows, cols] = jnp.where(low, d_k[0], d_k[1]).astype(jnp.bfloat16)
-        qkv[2, rows, cols] = jnp.where(low, d_v[0], d_v[1]).astype(jnp.bfloat16)
-        if j == 3:
-            hooks('dattn')
+    for s in range(tokens // SEQ):
+        @pl.loop(0, WIDE // PAIR)
+        def attend(j, s=s):
+            rows, cols = pair_block(s, j)
+            query, key, value = qkv[0, rows, cols], qkv[1, rows, cols], qkv[2, rows, cols]
+            d_ctx = ctx[rows, cols]
+            d_q, d_k, d_v = [], [], []
+            for h in range(2):
+                attn = probs[s, j, h]
+                d_probs = dot_bt(d_ctx * masks[h], value).astype(jnp.bfloat16).astype(jnp.float32)
+                d_v.append(dot_at(attn.astype(jnp.bfloat16), d_ctx))
+                inner = jnp.sum(d_probs * attn, axis=-1, keepdims=True)
+                d_scores = (attn * (d_probs - inner) * 0.125).astype(jnp.bfloat16)
+                d_q.append(dot(d_scores, key))
+                d_k.append(dot_at(d_scores, query))
+            qkv[0, rows, cols] = jnp.where(low, d_q[0], d_q[1]).astype(jnp.bfloat16)
+            qkv[1, rows, cols] = jnp.where(low, d_k[0], d_k[1]).astype(jnp.bfloat16)
+            qkv[2, rows, cols] = jnp.where(low, d_v[0], d_v[1]).astype(jnp.bfloat16)
+        hooks('dattn')
     low = low_half(tokens)
     for j in range(WIDE // PAIR):
         cols = pl.ds(j * PAIR, PAIR)
@@ -542,25 +549,6 @@
         for _ in range(count):
             next(gather, None)
 
-    gather_until(0)
-
-    def forward_hooks(layer):
-        counts = counts_of(GATHER_PUMPS[layer])
-
-        def hooks(name):
-            if name == 'out':
-                gather_until(3 * layer + 1)
-            elif name == 'up':
-                gather_until(3 * layer + 2)
-            else:
-                gather_pump(next(counts))
-        return hooks
-
-    hidden1[...] = layer_forward(0, x, weights, small, tab, saved, forward_hooks(0))
-    gather_until(3)
-    y_out[...] = layer_forward(1, hidden1, weights, small, tab, saved, forward_hooks(1))
-    gather_until(5)
-
     program = ScatterProgram()
 
     def add(layer, kind, lo):
@@ -587,8 +575,30 @@
                 add(self.layer, *chunk)
             program.pump(next(self.counts))
 
+    hooks1 = Hooks(1, SCATTER_PUMPS[0], False)
+    gather_until(0)
+
+    def forward_hooks(layer):
+        counts = counts_of(GATHER_PUMPS[layer])
+
+        def hooks(name):
+            if name == 'out':
+                gather_until(3 * layer + 1)
+            elif name == 'up':
+                if layer == 1:
+                    down_gradients(y_cot, act, down_g, hooks1)
+                gather_until(3 * layer + 2)
+            else:
+                gather_pump(next(counts))
+        return hooks
+
+    hidden1[...] = layer_forward(0, x, weights, small, tab, saved, forward_hooks(0))
+    gather_until(3)
+    y_out[...] = layer_forward(1, hidden1, weights, small, tab, saved, forward_hooks(1))
+    gather_until(5)
+
     d_hidden1[...] = layer_backward(1, hidden1, y_cot, weights, small, tab, saved, grads, small_grads,
-                                    Hooks(1, SCATTER_PUMPS[0], False))
+                                    hooks1)
     layer_forward(0, x, weights, small, tab, saved, Hooks(0, SCATTER_PUMPS[1], False))
     x_grad[...] = layer_backward(0, x, d_hidden1, weights, small, tab, saved, grads, small_grads,
                                  Hooks(0, SCATTER_PUMPS[2], True))

time: 189 us -> 188 us (level)
  Pallas kernels: 185 us -> 183 us
where the time goes in v4:
time: 188 us; the launch traced here: 187 us
  Pallas kernels  183 us (97%)
  local copies, waits for them, and re-layouts  3.41 us (2%)
    pallas_call x1, Pallas kernels, step_call(): pl.pallas_call(step_kernel, out_shape=(jax.ShapeDtypeStruct(x.shape, bf16...  181 us

profile of v4, /device:TPU:0, one launch (start us, length us, event | category | flops | bytes accessed | tf_op | source)
XLA Modules:
  0.0 187.3 jit_solution(16258651034788626967)
XLA Ops:
  0.6 1.7 reshape.48.qkv_own
  2.3 181.0 %shard_map.254 = (bf16[256,512]{1,0:T(8,128)(2,1)}, bf16[256,512]{1,0:T(8,128)(2,1)}, bf16[2,16,4096]{2,1,0:T(8,128)(2,1)}, bf16[2,64,512]{2,1,0:T(8,128)(2,1)}, f32[32,512]{1,0:T(8,128)}) custom-call(bf16[256,512]{1,0:T(8,128)(2,1)} %bitcast.6, bf16[256,512]{1,0:T(8,128)(2,1)} %bitcast.7, bf16[2,16,1536]{2,1,0:T(8,128)(2,1)} %reshape.48.qkv_own, ...), custom_call_target="tpu_custom_call" | custom-call | tf_op jit(solution)/shard_map/pallas_call | solution.py:625
  183.3 2.3 %shard_map.255 = (bf16[256,512]{1,0:T(8,128)(2,1)}, bf16[256,512]{1,0:T(8,128)(2,1)}, bf16[2,16]{1,0:T(2,128)(2,1)}, bf16[2,16]{1,0:T(2,128)(2,1)}, bf16[2,16,15...) custom-call(bf16[256,512]{1,0:T(8,128)(2,1)} %get-tuple-element.33.y, ...), custom_call_target="tpu_custom_call" | custom-call | tf_op jit(solution)/shard_map/pallas_call | solution.py:681
  185.6 1.7 reshape.51

commit v5 on v4

--- a/solution.py
+++ b/solution.py
@@ -363,7 +363,7 @@
     causal = (lax.broadcasted_iota(jnp.int32, (SEQ, SEQ), 0) >= lax.broadcasted_iota(jnp.int32, (SEQ, SEQ), 1))
     masks, low = head_masks(), low_half(SEQ)
     for s in range(tokens // SEQ):
-        @pl.loop(0, WIDE // PAIR)
+        @pl.loop(0, WIDE // PAIR, unroll=True)
         def attend(j, s=s):
             rows, cols = pair_block(s, j)
             query, key, value = qkv[0, rows, cols], qkv[1, rows, cols], qkv[2, rows, cols]
@@ -443,7 +443,7 @@
     hooks('dctx', (0, OUT))
     masks, low = head_masks(), low_half(SEQ)
     for s in range(tokens // SEQ):
-        @pl.loop(0, WIDE // PAIR)
+        @pl.loop(0, WIDE // PAIR, unroll=True)
         def attend(j, s=s):
             rows, cols = pair_block(s, j)
             query, key, value = qkv[0, rows, cols], qkv[1, rows, cols], qkv[2, rows, cols]

time: 188 us -> 185 us (0.984)
  Pallas kernels: 183 us -> 180 us
    pallas_call x1, Pallas kernels: 181 us -> 178 us  [step_call(): pl.pallas_call(step_kernel, out_shape=(jax.ShapeDtypeStruct(x.shape, bf16...]
where the time goes in v5:
time: 185 us; the launch traced here: 184 us
  Pallas kernels  180 us (97%)
  local copies, waits for them, and re-layouts  3.41 us (2%)
    pallas_call x1, Pallas kernels, step_call(): pl.pallas_call(step_kernel, out_shape=(jax.ShapeDtypeStruct(x.shape, bf16...  178 us

profile of v5, /device:TPU:0, one launch (start us, length us, event | category | flops | bytes accessed | tf_op | source)
XLA Modules:
  0.0 184.3 jit_solution(9802778980963763196)
XLA Ops:
  0.6 1.7 reshape.48.qkv_own
  2.3 177.9 %shard_map.254 = (bf16[256,512]{1,0:T(8,128)(2,1)}, bf16[256,512]{1,0:T(8,128)(2,1)}, bf16[2,16,4096]{2,1,0:T(8,128)(2,1)}, bf16[2,64,512]{2,1,0:T(8,128)(2,1)}, f32[32,512]{1,0:T(8,128)}) custom-call(bf16[256,512]{1,0:T(8,128)(2,1)} %bitcast.6, bf16[256,512]{1,0:T(8,128)(2,1)} %bitcast.7, bf16[2,16,1536]{2,1,0:T(8,128)(2,1)} %reshape.48.qkv_own, ...), custom_call_target="tpu_custom_call" | custom-call | tf_op jit(solution)/shard_map/pallas_call | solution.py:625
  180.2 2.3 %shard_map.255 = (bf16[256,512]{1,0:T(8,128)(2,1)}, bf16[256,512]{1,0:T(8,128)(2,1)}, bf16[2,16]{1,0:T(2,128)(2,1)}, bf16[2,16]{1,0:T(2,128)(2,1)}, bf16[2,16,15...) custom-call(bf16[256,512]{1,0:T(8,128)(2,1)} %get-tuple-element.33.y, ...), custom_call_target="tpu_custom_call" | custom-call | tf_op jit(solution)/shard_map/pallas_call | solution.py:681
  182.6 1.7 reshape.51
